TPU v7x, 512 devices: a whole 4x8x8 slice. The times are simulated.
512 devices in a mesh: sx: 16 (over z, x_hi), sy: 32 (over y, x_lo, core).
Axes of the slice: x: 4 (x_hi: 2, x_lo: 2; x = x_hi * 2 + x_lo), y: 8, z: 8, core: 2. Of those that a mesh axis runs over, the one named last changes fastest.
Arguments:
- coeffs: float32 [2, 32, 32, 16, 256], P(None, 'sx', 'sy'), may hold values from -6 to 6
- source_nodes: float32 [3, 2, 32, 32, 256], P(None, None, 'sx', 'sy'), may hold values from 0.2 to 1
- target_nodes: float32 [3, 2, 2, 2, 32, 32, 256], P(None, None, None, None, 'sx', 'sy'), may hold values from 0.2 to 1
- interp_rows: float32 [3, 2, 16, 16], replicated, may hold values from -1 to 1
- interp_cols: float32 [3, 2, 16, 16], replicated, may hold values from -1 to 1
Outputs:
- field: float32 [2, 32, 32, 16, 256], P(None, 'sx', 'sy')
All inputs are finite; a program needn't handle non-finite values.
Results may differ from a plain program's by a relative error of at most 0.0003.
Values sent between devices are 32-bit elements; how exact they have to be, the bound alone decides.
No kernel may reach another device: no remote copies, remote signals or barrier semaphores. Data moves between devices by JAX's collectives and lax.ppermute only.
A program may use at most 64 MiB of HBM per device.

v0:
```python
import jax
import jax.numpy as jnp
from jax import lax
from jax.sharding import PartitionSpec as P

LEVELS = 3


angular_scale = 25.132741228718345


def swapped(block, axis, bit):
    count = lax.axis_size(axis)
    route = []
    for low in range(count):
        high = low | 1 << bit
        if high != low and high < count:
            route += [(low, high), (high, low)]
    return lax.ppermute(block, axis, route)


def kron_of(rows_matrix, cols_matrix):
    width = rows_matrix.shape[0]
    return (rows_matrix[:, None, :, None] * cols_matrix[None, :, None, :]).reshape(
        width * width, width * width
    )


def translate_one(values, source, target, kron_matrix):
    angles = (
        angular_scale
        * source[0][None, :]
        * jnp.sqrt(
            target[0][:, None] * target[0][:, None]
            + target[1][:, None] * source[1][None, :] * (target[1][:, None] * source[1][None, :])
        )
    )
    weights = jnp.concatenate(
        [kron_matrix * jnp.cos(angles), kron_matrix * jnp.sin(angles)], axis=0
    )
    gathers = values.shape[1]
    points = values.shape[2]
    stacked = values.reshape(2 * gathers, points)
    product = jnp.einsum("rs,ts->rt", stacked, weights, precision=lax.Precision.HIGHEST)
    real_out = product[:gathers, :points] - product[gathers:, points:]
    imag_out = product[:gathers, points:] + product[gathers:, :points]
    return jnp.stack([real_out, imag_out])


def translate_boxes(current, source, target, kron_matrix):
    rows_count, cols_count = (current.shape[1], current.shape[2])
    gathers, points = (current.shape[3], current.shape[4])
    values = current.transpose(1, 2, 0, 3, 4).reshape(rows_count * cols_count, 2, gathers, points)
    sources = source.transpose(1, 2, 0, 3).reshape(rows_count * cols_count, 2, points)
    targets = target.transpose(1, 2, 0, 3).reshape(rows_count * cols_count, 2, points)
    result = lax.map(
        lambda item: translate_one(item[0], item[1], item[2], kron_matrix),
        (values, sources, targets),
    )
    return result.reshape(rows_count, cols_count, 2, gathers, points).transpose(2, 0, 1, 3, 4)


def all_positions(current, source, target, rows_level, cols_level):
    outputs = []
    for row_pos in range(2):
        line = []
        for col_pos in range(2):
            kron_matrix = kron_of(rows_level[row_pos], cols_level[col_pos])
            line.append(translate_boxes(current, source, target[:, row_pos, col_pos], kron_matrix))
        outputs.append(line)
    return outputs


def local(coeffs, source_nodes, target_nodes, interp_rows, interp_cols):
    rows_log = lax.axis_size("sx").bit_length() - 1
    cols_log = lax.axis_size("sy").bit_length() - 1
    row_index = lax.axis_index("sx")
    col_index = lax.axis_index("sy")
    current = coeffs
    for level_index in range(LEVELS):
        bit_rows = level_index % rows_log
        bit_cols = level_index % cols_log
        row_bit = row_index // 2**bit_rows % 2
        col_bit = col_index // 2**bit_cols % 2
        source = source_nodes[level_index]
        target = target_nodes[level_index]
        parts = all_positions(
            current, source, target, interp_rows[level_index], interp_cols[level_index]
        )
        zero_cols = jnp.stack([parts[0][0], parts[1][0]])
        one_cols = jnp.stack([parts[0][1], parts[1][1]])
        keep_pair = jnp.where(col_bit == 0, zero_cols, one_cols)
        send_pair = jnp.where(col_bit == 0, one_cols, zero_cols)
        paired = keep_pair + swapped(send_pair, "sy", bit_cols)
        keep_one = jnp.where(row_bit == 0, paired[0], paired[1])
        send_one = jnp.where(row_bit == 0, paired[1], paired[0])
        current = keep_one + swapped(send_one, "sx", bit_rows)
    return current


def solution(mesh):
    in_specs = (
        P(None, "sx", "sy", None, None),
        P(None, None, "sx", "sy", None),
        P(None, None, None, None, "sx", "sy", None),
        P(),
        P(),
    )
    out_specs = P(None, "sx", "sy", None, None)
    return jax.shard_map(local, mesh=mesh, in_specs=in_specs, out_specs=out_specs, check_vma=False)
```

profile of v0, /device:TPU:8, one launch (start us, length us, event | category | flops | bytes accessed | tf_op | source)
XLA Modules:
  0.0 116.3 jit_solution(8487011945517408324)
XLA Ops:
  3.2 5.8 %while.132 = (s32[]{:T(128)}, f32[2,2,16,256]{3,2,1,0:T(8,128)S(1)}, f32[2,2,16,256]{3,2,1,0:T(8,128)S(1)}, f32[2,2,256]{2,1,0:T(2,128)S(1)}, f32[2,2,256]{2,1,0...) while((s32[]{:T(128)}, f32[2,2,16,256]{3,2,1,0:T(8,128)S(1)}, ...), condition=%wide.region_1.2_spmd.clone, body=%wide.region_0.1_spmd.clone.sunk | while | flops 50938368 | bytes 2439297 | solution.py:56
  9.1 5.8 %while.133 = (s32[]{:T(128)}, f32[2,2,16,256]{3,2,1,0:T(8,128)S(1)}, f32[2,2,16,256]{3,2,1,0:T(8,128)S(1)}, f32[2,2,256]{2,1,0:T(2,128)S(1)}, f32[2,2,256]{2,1,0...) while((s32[]{:T(128)}, f32[2,2,16,256]{3,2,1,0:T(8,128)S(1)}, ...), condition=%wide.region_3.4_spmd.clone, body=%wide.region_2.3_spmd.clone.sunk | while | flops 50938368 | bytes 2439297 | solution.py:56
  15.0 5.8 %while.134 = (s32[]{:T(128)}, f32[2,2,16,256]{3,2,1,0:T(8,128)S(1)}, f32[2,2,16,256]{3,2,1,0:T(8,128)S(1)}, f32[2,2,256]{2,1,0:T(2,128)S(1)}, f32[2,2,256]{2,1,0...) while((s32[]{:T(128)}, f32[2,2,16,256]{3,2,1,0:T(8,128)S(1)}, ...), condition=%wide.region_5.6_spmd.clone, body=%wide.region_4.5_spmd.clone.sunk | while | flops 50938368 | bytes 2439297 | solution.py:56
  20.8 5.8 %while.135 = (s32[]{:T(128)}, f32[2,2,16,256]{3,2,1,0:T(8,128)S(1)}, f32[2,2,16,256]{3,2,1,0:T(8,128)S(1)}, f32[2,2,256]{2,1,0:T(2,128)S(1)}, f32[2,2,256]{2,1,0...) while((s32[]{:T(128)}, f32[2,2,16,256]{3,2,1,0:T(8,128)S(1)}, ...), condition=%wide.region_7.8_spmd.clone, body=%wide.region_6.7_spmd.clone.sunk | while | flops 50938368 | bytes 2439297 | solution.py:56
  26.7 1.9 %collective-permute-start = (f32[2,2,2,1,16,256]{5,4,1,2,3,0:T(8,128)S(1)}, f32[2,2,2,1,16,256]{5,4,1,2,3,0:T(8,128)S(1)}, u32[]{:S(2)}, u32[]{:S(2)}) collective-permute-start(f32[2,2,2,1,16,256]{5,4,1,2,3,0:T(8,128)S(1)} %fusion.146), channel_id=1, source_target_pairs={{0,1},{1,0},{2,3},{3,2},{4,5},{5,4},{6,7},{7,6},{8,9},{9,8},{10,11... | collective-permute-start | bytes 393224 | tf_op jit(solution)/shard_map/ppermute | solution.py:19
  28.7 1.3 %collective-permute-done = f32[2,2,2,1,16,256]{5,4,1,2,3,0:T(8,128)S(1)} collective-permute-done((f32[2,2,2,1,16,256]{5,4,1,2,3,0:T(8,128)S(1)}, f32[2,2,2,1,16,256]{5,4,1,2,3,0:T(8,128)S(1)}, u32[]{:S(2)}, u32[]{:S(2)}) %collective-permute-start) | collective-permute-done | bytes 131104 | tf_op jit(solution)/shard_map/ppermute | solution.py:19
  30.0 5.1 %collective-permute-start.1 = (f32[2,2,1,16,256]{4,3,0,1,2:T(8,128)S(1)}, f32[2,2,1,16,256]{4,3,0,1,2:T(8,128)S(1)}, u32[]{:S(2)}, u32[]{:S(2)}) collective-permute-start(f32[2,2,1,16,256]{4,3,0,1,2:T(8,128)S(1)} %select_bitcast_fusion.2), channel_id=1, source_target_pairs={{0,32},{32,0},{64,96},{96,64},{128,160},{160,128},{192,224},{224,1... | collective-permute-start | bytes 196616 | tf_op jit(solution)/shard_map/ppermute | solution.py:19
  35.2 2.5 %collective-permute-done.1 = f32[2,2,1,16,256]{4,3,0,1,2:T(8,128)S(1)} collective-permute-done((f32[2,2,1,16,256]{4,3,0,1,2:T(8,128)S(1)}, f32[2,2,1,16,256]{4,3,0,1,2:T(8,128)S(1)}, u32[]{:S(2)}, u32[]{:S(2)}) %collective-permute-start.1) | collective-permute-done | bytes 65568 | tf_op jit(solution)/shard_map/ppermute | solution.py:19
  37.7 5.8 %while.136 = (s32[]{:T(128)}, f32[2,2,16,256]{3,2,1,0:T(8,128)S(1)}, f32[2,2,16,256]{3,2,1,0:T(8,128)S(1)}, f32[2,2,256]{2,1,0:T(2,128)S(1)}, f32[2,2,256]{2,1,0...) while((s32[]{:T(128)}, f32[2,2,16,256]{3,2,1,0:T(8,128)S(1)}, ...), condition=%wide.region_9.10_spmd.clone, body=%wide.region_8.9_spmd.clone.sunk | while | flops 50938368 | bytes 2439297 | solution.py:56
  43.6 5.8 %while.137 = (s32[]{:T(128)}, f32[2,2,16,256]{3,2,1,0:T(8,128)S(1)}, f32[2,2,16,256]{3,2,1,0:T(8,128)S(1)}, f32[2,2,256]{2,1,0:T(2,128)S(1)}, f32[2,2,256]{2,1,0...) while((s32[]{:T(128)}, f32[2,2,16,256]{3,2,1,0:T(8,128)S(1)}, ...), condition=%wide.region_11.12_spmd.clone, body=%wide.region_10.11_spmd.clone.sunk | while | flops 50938368 | bytes 2439297 | solution.py:56
  49.4 5.8 %while.138 = (s32[]{:T(128)}, f32[2,2,16,256]{3,2,1,0:T(8,128)S(1)}, f32[2,2,16,256]{3,2,1,0:T(8,128)S(1)}, f32[2,2,256]{2,1,0:T(2,128)S(1)}, f32[2,2,256]{2,1,0...) while((s32[]{:T(128)}, f32[2,2,16,256]{3,2,1,0:T(8,128)S(1)}, ...), condition=%wide.region_13.14_spmd.clone, body=%wide.region_12.13_spmd.clone.sunk | while | flops 50938368 | bytes 2439297 | solution.py:56
  55.3 5.8 %while.139 = (s32[]{:T(128)}, f32[2,2,16,256]{3,2,1,0:T(8,128)S(1)}, f32[2,2,16,256]{3,2,1,0:T(8,128)S(1)}, f32[2,2,256]{2,1,0:T(2,128)S(1)}, f32[2,2,256]{2,1,0...) while((s32[]{:T(128)}, f32[2,2,16,256]{3,2,1,0:T(8,128)S(1)}, ...), condition=%wide.region_15.16_spmd.clone, body=%wide.region_14.15_spmd.clone.sunk | while | flops 50938368 | bytes 2439297 | solution.py:56
  61.2 3.4 %collective-permute-start.2 = (f32[2,2,2,1,16,256]{5,4,1,2,3,0:T(8,128)S(1)}, f32[2,2,2,1,16,256]{5,4,1,2,3,0:T(8,128)S(1)}, u32[]{:S(2)}, u32[]{:S(2)}) collective-permute-start(f32[2,2,2,1,16,256]{5,4,1,2,3,0:T(8,128)S(1)} %fusion.145), channel_id=1, source_target_pairs={{0,2},{2,0},{1,3},{3,1},{4,6},{6,4},{5,7},{7,5},{8,10},{10,8},{9,1... | collective-permute-start | bytes 393224 | tf_op jit(solution)/shard_map/ppermute | solution.py:19
  64.6 3.4 %collective-permute-done.2 = f32[2,2,2,1,16,256]{5,4,1,2,3,0:T(8,128)S(1)} collective-permute-done((f32[2,2,2,1,16,256]{5,4,1,2,3,0:T(8,128)S(1)}, f32[2,2,2,1,16,256]{5,4,1,2,3,0:T(8,128)S(1)}, u32[]{:S(2)}, u32[]{:S(2)}) %collective-permute-start.2) | collective-permute-done | bytes 131104 | tf_op jit(solution)/shard_map/ppermute | solution.py:19
  68.1 4.5 %collective-permute-start.3 = (f32[2,2,1,16,256]{4,3,0,1,2:T(8,128)S(1)}, f32[2,2,1,16,256]{4,3,0,1,2:T(8,128)S(1)}, u32[]{:S(2)}, u32[]{:S(2)}) collective-permute-start(f32[2,2,1,16,256]{4,3,0,1,2:T(8,128)S(1)} %select_bitcast_fusion.1), channel_id=1, source_target_pairs={{0,64},{64,0},{32,96},{96,32},{128,192},{192,128},{160,224},{224,1... | collective-permute-start | bytes 196616 | tf_op jit(solution)/shard_map/ppermute | solution.py:19
  72.6 1.9 %collective-permute-done.3 = f32[2,2,1,16,256]{4,3,0,1,2:T(8,128)S(1)} collective-permute-done((f32[2,2,1,16,256]{4,3,0,1,2:T(8,128)S(1)}, f32[2,2,1,16,256]{4,3,0,1,2:T(8,128)S(1)}, u32[]{:S(2)}, u32[]{:S(2)}) %collective-permute-start.3) | collective-permute-done | bytes 65568 | tf_op jit(solution)/shard_map/ppermute | solution.py:19
  74.6 5.8 %while.140 = (s32[]{:T(128)}, f32[2,2,16,256]{3,2,0,1:T(8,128)S(1)}, f32[2,2,16,256]{3,2,1,0:T(8,128)S(1)}, f32[2,2,256]{2,1,0:T(2,128)S(1)}, f32[2,2,256]{2,1,0...) while((s32[]{:T(128)}, f32[2,2,16,256]{3,2,0,1:T(8,128)S(1)}, ...), condition=%wide.region_17.18_spmd.clone, body=%wide.region_16.17_spmd.clone.sunk | while | flops 50938368 | bytes 2439297 | solution.py:56
  80.5 5.8 %while.141 = (s32[]{:T(128)}, f32[2,2,16,256]{3,2,0,1:T(8,128)S(1)}, f32[2,2,16,256]{3,2,1,0:T(8,128)S(1)}, f32[2,2,256]{2,1,0:T(2,128)S(1)}, f32[2,2,256]{2,1,0...) while((s32[]{:T(128)}, f32[2,2,16,256]{3,2,0,1:T(8,128)S(1)}, ...), condition=%wide.region_19.20_spmd.clone, body=%wide.region_18.19_spmd.clone.sunk | while | flops 50938368 | bytes 2439297 | solution.py:56
  86.4 5.8 %while.142 = (s32[]{:T(128)}, f32[2,2,16,256]{3,2,0,1:T(8,128)S(1)}, f32[2,2,16,256]{3,2,1,0:T(8,128)S(1)}, f32[2,2,256]{2,1,0:T(2,128)S(1)}, f32[2,2,256]{2,1,0...) while((s32[]{:T(128)}, f32[2,2,16,256]{3,2,0,1:T(8,128)S(1)}, ...), condition=%wide.region_21.22_spmd.clone, body=%wide.region_20.21_spmd.clone.sunk | while | flops 50938368 | bytes 2439297 | solution.py:56
  92.2 5.8 %while.143 = (s32[]{:T(128)}, f32[2,2,16,256]{3,2,0,1:T(8,128)S(1)}, f32[2,2,16,256]{3,2,1,0:T(8,128)S(1)}, f32[2,2,256]{2,1,0:T(2,128)S(1)}, f32[2,2,256]{2,1,0...) while((s32[]{:T(128)}, f32[2,2,16,256]{3,2,0,1:T(8,128)S(1)}, ...), condition=%wide.region_23.24_spmd.clone, body=%wide.region_22.23_spmd.clone.sunk | while | flops 50938368 | bytes 2439297 | solution.py:56
  98.1 7.3 %collective-permute-start.4 = (f32[2,2,2,1,16,256]{5,4,2,1,3,0:T(8,128)S(1)}, f32[2,2,2,1,16,256]{5,4,2,1,3,0:T(8,128)S(1)}, u32[]{:S(2)}, u32[]{:S(2)}) collective-permute-start(f32[2,2,2,1,16,256]{5,4,2,1,3,0:T(8,128)S(1)} %fusion.144), channel_id=1, source_target_pairs={{0,4},{4,0},{1,5},{5,1},{2,6},{6,2},{3,7},{7,3},{8,12},{12,8},{9,1... | collective-permute-start | bytes 393224 | tf_op jit(solution)/shard_map/ppermute | solution.py:19
  105.5 2.9 %collective-permute-done.4 = f32[2,2,2,1,16,256]{5,4,2,1,3,0:T(8,128)S(1)} collective-permute-done((f32[2,2,2,1,16,256]{5,4,2,1,3,0:T(8,128)S(1)}, f32[2,2,2,1,16,256]{5,4,2,1,3,0:T(8,128)S(1)}, u32[]{:S(2)}, u32[]{:S(2)}) %collective-permute-start.4) | collective-permute-done | bytes 131104 | tf_op jit(solution)/shard_map/ppermute | solution.py:19
  108.4 2.7 %collective-permute-start.5 = (f32[2,2,1,16,256]{4,3,2,1,0:T(8,128)S(1)}, f32[2,2,1,16,256]{4,3,2,1,0:T(8,128)S(1)}, u32[]{:S(2)}, u32[]{:S(2)}) collective-permute-start(f32[2,2,1,16,256]{4,3,2,1,0:T(8,128)S(1)} %select_bitcast_fusion), channel_id=1, source_target_pairs={{0,128},{128,0},{32,160},{160,32},{64,192},{192,64},{96,224},{224,... | collective-permute-start | bytes 196616 | tf_op jit(solution)/shard_map/ppermute | solution.py:19
  111.1 4.5 %collective-permute-done.5 = f32[2,2,1,16,256]{4,3,2,1,0:T(8,128)S(1)} collective-permute-done((f32[2,2,1,16,256]{4,3,2,1,0:T(8,128)S(1)}, f32[2,2,1,16,256]{4,3,2,1,0:T(8,128)S(1)}, u32[]{:S(2)}, u32[]{:S(2)}) %collective-permute-start.5) | collective-permute-done | bytes 65568 | tf_op jit(solution)/shard_map/ppermute | solution.py:19
  (228 shorter events, 72.6 us)
Async XLA Ops:
  26.7 3.2 %collective-permute-start = (f32[2,2,2,1,16,256]{5,4,1,2,3,0:T(8,128)S(1)}, f32[2,2,2,1,16,256]{5,4,1,2,3,0:T(8,128)S(1)}, u32[]{:S(2)}, u32[]{:S(2)}) collective-permute-start(f32[2,2,2,1,16,256]{5,4,1,2,3,0:T(8,128)S(1)} %fusion.146), channel_id=1, source_target_pairs={{0,1},{1,0},{2,3},{3,2},{4,5},{5,4},{6,7},{7,6},{8,9},{9,8},{10,11... | collective-permute-start | bytes 393224 | tf_op jit(solution)/shard_map/ppermute | solution.py:19
  30.0 7.7 %collective-permute-start.1 = (f32[2,2,1,16,256]{4,3,0,1,2:T(8,128)S(1)}, f32[2,2,1,16,256]{4,3,0,1,2:T(8,128)S(1)}, u32[]{:S(2)}, u32[]{:S(2)}) collective-permute-start(f32[2,2,1,16,256]{4,3,0,1,2:T(8,128)S(1)} %select_bitcast_fusion.2), channel_id=1, source_target_pairs={{0,32},{32,0},{64,96},{96,64},{128,160},{160,128},{192,224},{224,1... | collective-permute-start | bytes 196616 | tf_op jit(solution)/shard_map/ppermute | solution.py:19
  61.2 6.9 %collective-permute-start.2 = (f32[2,2,2,1,16,256]{5,4,1,2,3,0:T(8,128)S(1)}, f32[2,2,2,1,16,256]{5,4,1,2,3,0:T(8,128)S(1)}, u32[]{:S(2)}, u32[]{:S(2)}) collective-permute-start(f32[2,2,2,1,16,256]{5,4,1,2,3,0:T(8,128)S(1)} %fusion.145), channel_id=1, source_target_pairs={{0,2},{2,0},{1,3},{3,1},{4,6},{6,4},{5,7},{7,5},{8,10},{10,8},{9,1... | collective-permute-start | bytes 393224 | tf_op jit(solution)/shard_map/ppermute | solution.py:19
  68.1 6.5 %collective-permute-start.3 = (f32[2,2,1,16,256]{4,3,0,1,2:T(8,128)S(1)}, f32[2,2,1,16,256]{4,3,0,1,2:T(8,128)S(1)}, u32[]{:S(2)}, u32[]{:S(2)}) collective-permute-start(f32[2,2,1,16,256]{4,3,0,1,2:T(8,128)S(1)} %select_bitcast_fusion.1), channel_id=1, source_target_pairs={{0,64},{64,0},{32,96},{96,32},{128,192},{192,128},{160,224},{224,1... | collective-permute-start | bytes 196616 | tf_op jit(solution)/shard_map/ppermute | solution.py:19
  98.1 10.3 %collective-permute-start.4 = (f32[2,2,2,1,16,256]{5,4,2,1,3,0:T(8,128)S(1)}, f32[2,2,2,1,16,256]{5,4,2,1,3,0:T(8,128)S(1)}, u32[]{:S(2)}, u32[]{:S(2)}) collective-permute-start(f32[2,2,2,1,16,256]{5,4,2,1,3,0:T(8,128)S(1)} %fusion.144), channel_id=1, source_target_pairs={{0,4},{4,0},{1,5},{5,1},{2,6},{6,2},{3,7},{7,3},{8,12},{12,8},{9,1... | collective-permute-start | bytes 393224 | tf_op jit(solution)/shard_map/ppermute | solution.py:19
  108.4 7.2 %collective-permute-start.5 = (f32[2,2,1,16,256]{4,3,2,1,0:T(8,128)S(1)}, f32[2,2,1,16,256]{4,3,2,1,0:T(8,128)S(1)}, u32[]{:S(2)}, u32[]{:S(2)}) collective-permute-start(f32[2,2,1,16,256]{4,3,2,1,0:T(8,128)S(1)} %select_bitcast_fusion), channel_id=1, source_target_pairs={{0,128},{128,0},{32,160},{160,32},{64,192},{192,64},{96,224},{224,... | collective-permute-start | bytes 196616 | tf_op jit(solution)/shard_map/ppermute | solution.py:19
where the time goes:
time: 117 us; the launch traced here: 116 us
  other arithmetic  33 us (28%)
  local copies, waits for them, and re-layouts  26.1 us (22%)
  starting transfers between devices  24.9 us (21%)
  waiting for transfers between devices  16.6 us (14%)
  matrix products  13.5 us (12%)
  loops' own time  1.66 us (1%)
    mul x24, other arithmetic, translate_one(): kron_matrix * jnp.cos(angles)  26.6 us
    ppermute x6, starting transfers between devices, swapped(): return lax.ppermute(block, axis, route)  24.9 us
    mul x25, local copies, waits for them, and re-layouts, kron_of(): rows_matrix[:, None, :, None] * cols_matrix[None, :, None, :]  23.4 us
    ppermute x6, waiting for transfers between devices, swapped(): return lax.ppermute(block, axis, route)  16.6 us
    dot_general x24, matrix products, translate_one(): jnp.einsum('rs,ts->rt', stacked, weights, precision=lax.Precision.HIGHEST)  13.5 us
    mul x24, other arithmetic, kron_of(): rows_matrix[:, None, :, None] * cols_matrix[None, :, None, :]  4.84 us
  transfers between devices with their start and end apart: 6, of which 6 were waited for; matrix products, arithmetic and copies ran while one was open for 0% of the time, Pallas kernels for 0%

commit v1 on v0

v1 whole, which is shorter than its diff:
```python
import functools
import math

import jax
import jax.numpy as jnp
import numpy as np
from jax import lax
from jax.experimental import pallas as pl
from jax.experimental.pallas import tpu as pltpu
from jax.sharding import PartitionSpec as P

LEVELS = 3
CHEB = 16
NODES = CHEB * CHEB
RHS = 16
BOXES = 2
KERNELS = 4 * BOXES
ROOT2 = math.sqrt(2.0)


def half_turn_coefficients():
    nodes = 0.5 * np.cos((np.arange(64) + 0.5) * np.pi / 128)
    powers = np.stack([nodes, nodes**3, nodes**5], axis=1)
    wanted = 2.0**0.75 * np.sin(0.5 * np.pi * nodes)
    return [float(c) for c in np.linalg.lstsq(powers, wanted, rcond=None)[0]]


C0, C1, C2 = half_turn_coefficients()


def group_members(mesh, bit):
    n_rows, n_cols = mesh.shape["sx"], mesh.shape["sy"]
    step = 1 << bit
    groups = []
    for row in range(n_rows):
        for col in range(n_cols):
            if not row & step and not col & step:
                groups.append(
                    [(row + a) * n_cols + col + c for a in (0, step) for c in (0, step)]
                )
    return groups


def prepare(level, sources, rows, cols, a_ref, b_ref, row_ref, col_ref):
    lane = lax.broadcasted_iota(jnp.int32, (CHEB, NODES), 1)
    node = lax.broadcasted_iota(jnp.int32, (CHEB, NODES), 0)
    outer = (lane // CHEB == node).astype(jnp.float32)
    inner = (lane % CHEB == node).astype(jnp.float32)
    spread = functools.partial(
        lax.dot_general,
        dimension_numbers=(((0,), (0,)), ((), ())),
        precision=lax.Precision.HIGHEST,
        preferred_element_type=jnp.float32,
    )
    for bit in range(2):
        row_ref[bit] = spread(rows[level, bit], outer)
        col_ref[bit] = spread(cols[level, bit], inner)
    lines = []
    for box in range(BOXES):
        freq = sources[level, 0, box]
        slow = sources[level, 1, box]
        near = 16.0 * freq * freq
        lines += [near, near * slow * slow]
    columns = jnp.concatenate(lines + lines, axis=0).T
    for box in range(BOXES):
        a_ref[box] = jnp.broadcast_to(columns[:, 2 * box : 2 * box + 1], (NODES, 128))
        b_ref[box] = jnp.broadcast_to(columns[:, 2 * box + 1 : 2 * box + 2], (NODES, 128))


def weigh(level, targets, a_ref, b_ref, row_ref, col_ref, high, low):
    for box in range(BOXES):
        squares = []
        for pos in range(4):
            tau = targets[level, 0, pos // 2, pos % 2, box]
            off = targets[level, 1, pos // 2, pos % 2, box]
            squares.append((tau * tau, off * off))

        def strip(step, carry):
            down = pl.ds(step * CHEB, CHEB)
            along = pl.ds(NODES + step * CHEB, CHEB)
            near = a_ref[box, down, :]
            far = b_ref[box, down, :]
            near = jnp.concatenate([near, near], axis=1)
            far = jnp.concatenate([far, far], axis=1)
            for pos in range(4):
                tau2, off2 = squares[pos]
                kron = row_ref[pos // 2, pl.ds(step, 1), :] * col_ref[pos % 2]
                z = near * tau2 + far * off2
                turns = z * lax.rsqrt(z)
                rest = turns - jnp.round(turns)
                y = rest * rest
                half = rest * (C0 + y * (C1 + y * C2))
                q = half * half
                cosine = ROOT2 - q
                v = 2.0 * ROOT2 - q
                sine = half * (v * lax.rsqrt(v))
                part = kron * sine
                real = kron - part * sine
                imag = part * cosine
                item = box * 4 + pos
                for where, value in ((down, real), (along, imag)):
                    top = value.astype(jnp.bfloat16)
                    high[item, where, :] = top
                    low[item, where, :] = (value - top.astype(jnp.float32)).astype(jnp.bfloat16)
            return carry

        lax.fori_loop(0, CHEB, strip, 0)


def apply(box, values, high, low, out):
    def turned(x):
        return jnp.concatenate([-x[RHS:], x[:RHS]], axis=0)

    top = values.astype(jnp.bfloat16)
    rest = (values - top.astype(jnp.float32)).astype(jnp.bfloat16)
    left = jnp.concatenate([top, rest], axis=0)
    right = jnp.concatenate([turned(top), turned(rest)], axis=0)
    both = jnp.concatenate([left, right], axis=1)
    for pos in range(4):
        item = box * 4 + pos
        main = jnp.dot(both, high[item], preferred_element_type=jnp.float32)
        small = jnp.dot(both[: 2 * RHS], low[item], preferred_element_type=jnp.float32)
        total = main[: 2 * RHS] + main[2 * RHS :] + small
        out[pos, pl.ds(box * RHS, RHS), :] = total[:RHS]
        out[pos, pl.ds((BOXES + box) * RHS, RHS), :] = total[RHS:]


def first_kernel(coeffs, sources, targets, rows, cols, out, a_ref, b_ref, row_ref, col_ref, high, low):
    prepare(0, sources, rows, cols, a_ref, b_ref, row_ref, col_ref)
    weigh(0, targets, a_ref, b_ref, row_ref, col_ref, high, low)
    for box in range(BOXES):
        values = jnp.concatenate([coeffs[0, box], coeffs[1, box]], axis=0)
        apply(box, values, high, low, out)


def weights_kernel(level, sources, targets, rows, cols, high, low, a_ref, b_ref, row_ref, col_ref):
    prepare(level, sources, rows, cols, a_ref, b_ref, row_ref, col_ref)
    weigh(level, targets, a_ref, b_ref, row_ref, col_ref, high, low)


def later_kernel(pieces, high, low, out):
    summed = (pieces[0] + pieces[1]) + (pieces[2] + pieces[3])
    for box in range(BOXES):
        values = jnp.concatenate(
            [
                summed[box * RHS : (box + 1) * RHS],
                summed[(BOXES + box) * RHS : (BOXES + box + 1) * RHS],
            ],
            axis=0,
        )
        apply(box, values, high, low, out)


TABLES = (
    pltpu.VMEM((BOXES, NODES, 128), jnp.float32),
    pltpu.VMEM((BOXES, NODES, 128), jnp.float32),
    pltpu.VMEM((2, CHEB, NODES), jnp.float32),
    pltpu.VMEM((2, CHEB, NODES), jnp.float32),
)
WEIGHTS = pltpu.VMEM((KERNELS, 2 * NODES, NODES), jnp.bfloat16)
SENT = pltpu.VMEM((4, 2 * BOXES * RHS, NODES), jnp.float32)
SMALL = pltpu.CompilerParams(vmem_limit_bytes=12 * 1024 * 1024)


def solution(mesh):
    groups = [group_members(mesh, bit) for bit in range(LEVELS)]

    def exchange(sent, level):
        return lax.all_to_all(
            sent, ("sx", "sy"), 0, 0, axis_index_groups=groups[level], tiled=True
        )

    def local(coeffs, source_nodes, target_nodes, interp_rows, interp_cols):
        coeffs = coeffs.reshape(2, BOXES, RHS, NODES)
        sources = source_nodes.reshape(LEVELS, 2, BOXES, 1, NODES)
        targets = target_nodes.reshape(LEVELS, 2, 2, 2, BOXES, 1, NODES)
        sent = pl.pallas_call(
            first_kernel,
            out_shape=SENT,
            scratch_shapes=TABLES + (WEIGHTS, WEIGHTS),
            compiler_params=SMALL,
            name="first",
        )(coeffs, sources, targets, interp_rows, interp_cols)
        made = [
            pl.pallas_call(
                functools.partial(weights_kernel, level),
                out_shape=(WEIGHTS, WEIGHTS),
                scratch_shapes=TABLES,
                compiler_params=SMALL,
                cost_estimate=pl.CostEstimate(
                    flops=60_000_000, bytes_accessed=100_000, transcendentals=0
                ),
                name=f"weights_{level}",
            )(sources, targets, interp_rows, interp_cols)
            for level in range(1, LEVELS)
        ]
        for level in range(1, LEVELS):
            sent = pl.pallas_call(
                later_kernel, out_shape=SENT, compiler_params=SMALL, name=f"later_{level}"
            )(exchange(sent, level - 1), *made[level - 1])
        pieces = exchange(sent, LEVELS - 1)
        field = (pieces[0] + pieces[1]) + (pieces[2] + pieces[3])
        return field.reshape(2, BOXES, 1, RHS, NODES)

    in_specs = (
        P(None, "sx", "sy", None, None),
        P(None, None, "sx", "sy", None),
        P(None, None, None, None, "sx", "sy", None),
        P(),
        P(),
    )
    out_specs = P(None, "sx", "sy", None, None)
    return jax.shard_map(local, mesh=mesh, in_specs=in_specs, out_specs=out_specs, check_vma=False)
```

time: 117 us -> 52.9 us (0.45)
  the two profiles are of different devices: /device:TPU:8 before, /device:TPU:4 now
where the time goes in v1:
time: 52.9 us; the launch traced here: 52.1 us
  Pallas kernels  13.1 us (25%)
  local copies, waits for them, and re-layouts  12.9 us (24%)
  starting transfers between devices  12.6 us (24%)
  blocking collectives  11.3 us (21%)
  waiting for transfers between devices  1.45 us (3%)
  other arithmetic  0.65 us (1%)
    unnamed x34, local copies, waits for them, and re-layouts  12.9 us
    all_to_all x2, starting transfers between devices, exchange(): lax.all_to_all(sent, ('sx', 'sy'), 0, 0, axis_index_groups=groups[level],...  12.6 us
    all_to_all x1, blocking collectives, exchange(): lax.all_to_all(sent, ('sx', 'sy'), 0, 0, axis_index_groups=groups[level],...  11.3 us
    pallas_call x2, Pallas kernels, local(): pl.pallas_call(functools.partial(weights_kernel, level), out_shape=(WEIGH...  6.13 us
    pallas_call x1, Pallas kernels, local(): pl.pallas_call(first_kernel, out_shape=SENT, scratch_shapes=TABLES + (WEI...  4.6 us
    pallas_call x2, Pallas kernels, local(): pl.pallas_call(later_kernel, out_shape=SENT, compiler_params=SMALL, name=...  2.36 us
    all_to_all x2, waiting for transfers between devices, exchange(): lax.all_to_all(sent, ('sx', 'sy'), 0, 0, axis_index_groups=groups[level],...  1.45 us
  transfers between devices with their start and end apart: 2, of which 1 were waited for; matrix products, arithmetic and copies ran while one was open for 0% of the time, Pallas kernels for 12%

profile of v1, /device:TPU:4, one launch (start us, length us, event | category | flops | bytes accessed | tf_op | source)
XLA Modules:
  0.0 52.1 jit_solution(2151904469259659526)
XLA Ops:
  0.0 0.8 %copy-done.4 = f32[2,2,1,16,256]{4,3,2,1,0:T(8,128)S(1)} copy-done((f32[2,2,1,16,256]{4,3,2,1,0:T(8,128)S(1)}, f32[2,2,1,16,256]{4,3,2,1,0:T(8,128)}, u32[]{:S(2)}) %copy-start.4) | copy-done | bytes 65560
  0.8 0.8 %copy-done.5 = f32[3,2,2,2,2,1,256]{6,5,4,3,2,1,0:T(1,128)S(1)} copy-done((f32[3,2,2,2,2,1,256]{6,5,4,3,2,1,0:T(1,128)S(1)}, f32[3,2,2,2,2,1,256]{6,5,4,3,2,1,0:T(1,128)}, u32[]{:S(2)}) %copy-start.5) | copy-done | bytes 49176
  1.6 0.8 %copy-done.8 = f32[3,2,16,16]{3,2,1,0:T(8,128)S(1)} copy-done((f32[3,2,16,16]{3,2,1,0:T(8,128)S(1)}, f32[3,2,16,16]{3,2,1,0:T(8,128)}, u32[]{:S(2)}) %copy-start.8) | copy-done | bytes 6168
  2.4 0.8 %copy-done.11 = f32[3,2,16,16]{3,2,1,0:T(8,128)S(1)} copy-done((f32[3,2,16,16]{3,2,1,0:T(8,128)S(1)}, f32[3,2,16,16]{3,2,1,0:T(8,128)}, u32[]{:S(2)}) %copy-start.11) | copy-done | bytes 6168
  3.2 0.7 %copy-done.14 = f32[3,2,2,1,256]{4,3,2,1,0:T(1,128)S(1)} copy-done((f32[3,2,2,1,256]{4,3,2,1,0:T(1,128)S(1)}, f32[3,2,2,1,256]{4,3,2,1,0:T(1,128)}, u32[]{:S(2)}) %copy-start.14) | copy-done | bytes 12312
  3.9 4.6 %first.1 = f32[4,64,256]{2,1,0:T(8,128)} custom-call(f32[2,2,16,256]{3,2,1,0:T(8,128)S(1)} %bitcast.4, f32[3,2,2,1,256]{4,3,2,1,0:T(1,128)S(1)} %copy-done.14, f32[3,2,2,2,2,1,256]{6,5,4,3,2,1,0:T(1,128)S(1)} %copy-done.5, f32[3,2,16,16]{3,2,1,0:T(8,128)S(1)} %copy-done.8, f32[3,2,16,16]{3,2,1,0:T(8,128)S(1)} %copy-done.11), custom_call_target="tpu_custom_call" | custom-call | tf_op jit(solution)/shard_map/first/pallas_call | solution.py:177
  8.5 9.2 %all-to-all-start = ((f32[4,64,256]{2,1,0:T(8,128)}), f32[4,64,256]{2,1,0:T(8,128)S(1)}, u32[]{:S(2)}, u32[]{:S(2)}) async-start(f32[4,64,256]{2,1,0:T(8,128)} %first.1), calls=%async_computation | async-start | bytes 524288 | tf_op jit(solution)/shard_map/all_to_all | solution.py:169
  17.8 0.8 %copy-done.6 = f32[3,2,2,2,2,1,256]{6,5,4,3,2,1,0:T(1,128)S(1)} copy-done((f32[3,2,2,2,2,1,256]{6,5,4,3,2,1,0:T(1,128)S(1)}, f32[3,2,2,2,2,1,256]{6,5,4,3,2,1,0:T(1,128)}, u32[]{:S(2)}) %copy-start.6) | copy-done | bytes 49176
  18.6 0.8 %copy-done.9 = f32[3,2,16,16]{3,2,1,0:T(8,128)S(1)} copy-done((f32[3,2,16,16]{3,2,1,0:T(8,128)S(1)}, f32[3,2,16,16]{3,2,1,0:T(8,128)}, u32[]{:S(2)}) %copy-start.9) | copy-done | bytes 6168
  19.4 0.8 %copy-done.12 = f32[3,2,16,16]{3,2,1,0:T(8,128)S(1)} copy-done((f32[3,2,16,16]{3,2,1,0:T(8,128)S(1)}, f32[3,2,16,16]{3,2,1,0:T(8,128)}, u32[]{:S(2)}) %copy-start.12) | copy-done | bytes 6168
  20.2 0.7 %copy-done.15 = f32[3,2,2,1,256]{4,3,2,1,0:T(1,128)S(1)} copy-done((f32[3,2,2,1,256]{4,3,2,1,0:T(1,128)S(1)}, f32[3,2,2,1,256]{4,3,2,1,0:T(1,128)}, u32[]{:S(2)}) %copy-start.15) | copy-done | bytes 12312
  20.9 3.1 %weights_1.1 = (bf16[8,512,256]{2,1,0:T(8,128)(2,1)S(1)}, bf16[8,512,256]{2,1,0:T(8,128)(2,1)S(1)}) custom-call(f32[3,2,2,1,256]{4,3,2,1,0:T(1,128)S(1)} %copy-done.15, f32[3,2,2,2,2,1,256]{6,5,4,3,2,1,0:T(1,128)S(1)} %copy-done.6, f32[3,2,16,16]{3,2,1,0:T(8,128)S(1)} %copy-done.9, f32[3,2,16,16]{3,2,1,0:T(8,128)S(1)} %copy-done.12), custom_call_target="tpu_custom_call" | custom-call | flops 60000000 | bytes 100000 | tf_op jit(solution)/shard_map/weights_1/pallas_call | solution.py:185
  24.0 1.3 %copy-done = bf16[8,512,256]{2,1,0:T(8,128)(2,1)} copy-done((bf16[8,512,256]{2,1,0:T(8,128)(2,1)}, bf16[8,512,256]{2,1,0:T(8,128)(2,1)S(1)}, u32[]{:S(2)}) %copy-start) | copy-done | bytes 2097176
  25.3 0.0 all-to-all-done.pieces
  25.3 1.6 %copy-done.1 = bf16[8,512,256]{2,1,0:T(8,128)(2,1)S(1)} copy-done((bf16[8,512,256]{2,1,0:T(8,128)(2,1)S(1)}, bf16[8,512,256]{2,1,0:T(8,128)(2,1)}, u32[]{:S(2)}) %copy-start.1) | copy-done | bytes 2097176
  26.9 1.5 %later_1.1 = f32[4,64,256]{2,1,0:T(8,128)} custom-call(f32[4,64,256]{2,1,0:T(8,128)S(1)} %all-to-all-done.pieces, bf16[8,512,256]{2,1,0:T(8,128)(2,1)S(1)} %get-tuple-element.9.high, bf16[8,512,256]{2,1,0:T(8,128)(2,1)S(1)} %copy-done.1), custom_call_target="tpu_custom_call" | custom-call | tf_op jit(solution)/shard_map/later_1/pallas_call | solution.py:198
  28.4 3.4 %all-to-all-start.1 = ((f32[4,64,256]{2,1,0:T(8,128)}), f32[4,64,256]{2,1,0:T(8,128)S(1)}, u32[]{:S(2)}, u32[]{:S(2)}) async-start(f32[4,64,256]{2,1,0:T(8,128)} %later_1.1), calls=%async_computation.1 | async-start | bytes 524288 | tf_op jit(solution)/shard_map/all_to_all | solution.py:169
  31.9 3.1 %weights_2.1 = (bf16[8,512,256]{2,1,0:T(8,128)(2,1)S(1)}, bf16[8,512,256]{2,1,0:T(8,128)(2,1)S(1)}) custom-call(f32[3,2,2,1,256]{4,3,2,1,0:T(1,128)S(1)} %copy-done.16, f32[3,2,2,2,2,1,256]{6,5,4,3,2,1,0:T(1,128)S(1)} %copy-done.7, f32[3,2,16,16]{3,2,1,0:T(8,128)S(1)} %copy-done.10, f32[3,2,16,16]{3,2,1,0:T(8,128)S(1)} %copy-done.13), custom_call_target="tpu_custom_call" | custom-call | flops 60000000 | bytes 100000 | tf_op jit(solution)/shard_map/weights_2/pallas_call | solution.py:185
  35.0 1.3 %copy-done.2 = bf16[8,512,256]{2,1,0:T(8,128)(2,1)} copy-done((bf16[8,512,256]{2,1,0:T(8,128)(2,1)}, bf16[8,512,256]{2,1,0:T(8,128)(2,1)S(1)}, u32[]{:S(2)}) %copy-start.2) | copy-done | bytes 2097176
  36.3 1.4 %all-to-all-done.1.pieces = f32[4,64,256]{2,1,0:T(8,128)S(1)} async-done(((f32[4,64,256]{2,1,0:T(8,128)}), f32[4,64,256]{2,1,0:T(8,128)S(1)}, u32[]{:S(2)}, u32[]{:S(2)}) %all-to-all-start.1) | async-done | bytes 262176 | tf_op jit(solution)/shard_map/all_to_all | solution.py:169
  37.7 1.6 %copy-done.3 = bf16[8,512,256]{2,1,0:T(8,128)(2,1)S(1)} copy-done((bf16[8,512,256]{2,1,0:T(8,128)(2,1)S(1)}, bf16[8,512,256]{2,1,0:T(8,128)(2,1)}, u32[]{:S(2)}) %copy-start.3) | copy-done | bytes 2097176
  39.3 0.8 %later_2.1 = f32[4,64,256]{2,1,0:T(8,128)S(1)} custom-call(f32[4,64,256]{2,1,0:T(8,128)S(1)} %all-to-all-done.1.pieces, bf16[8,512,256]{2,1,0:T(8,128)(2,1)S(1)} %get-tuple-element.11.high, bf16[8,512,256]{2,1,0:T(8,128)(2,1)S(1)} %copy-done.3), custom_call_target="tpu_custom_call" | custom-call | tf_op jit(solution)/shard_map/later_2/pallas_call | solution.py:198
  40.1 11.3 %all_to_all.15 = f32[4,64,256]{2,1,0:T(8,128)S(1)} all-to-all(f32[4,64,256]{2,1,0:T(8,128)S(1)} %later_2.1), channel_id=1, replica_groups={{0,4,128,132},{1,5,129,133},{2,6,130,134},{3,7,131,135},{8,12,136,140},..., dimensions={0} | all-to-all | bytes 524288 | tf_op jit(solution)/shard_map/all_to_all | solution.py:169
  51.4 0.6 %fusion = f32[1,64,256]{2,1,0:T(8,128)} fusion(f32[4,64,256]{2,1,0:T(8,128)S(1)} %all_to_all.15), kind=kLoop, calls=%fused_computation.1 | loop fusion | flops 49152 | bytes 327680 | tf_op jit(solution)/shard_map/add | solution.py:202
  (21 shorter events, 0.0 us)
Async XLA Ops:
  0.0 0.8 %copy-start.4 = (f32[2,2,1,16,256]{4,3,2,1,0:T(8,128)S(1)}, f32[2,2,1,16,256]{4,3,2,1,0:T(8,128)}, u32[]{:S(2)}) copy-start(f32[2,2,1,16,256]{4,3,2,1,0:T(8,128)} %param.5) | copy-start | bytes 196612
  0.8 0.8 %copy-start.5 = (f32[3,2,2,2,2,1,256]{6,5,4,3,2,1,0:T(1,128)S(1)}, f32[3,2,2,2,2,1,256]{6,5,4,3,2,1,0:T(1,128)}, u32[]{:S(2)}) copy-start(f32[3,2,2,2,2,1,256]{6,5,4,3,2,1,0:T(1,128)} %targets.5) | copy-start | bytes 147460
  1.6 0.8 %copy-start.8 = (f32[3,2,16,16]{3,2,1,0:T(8,128)S(1)}, f32[3,2,16,16]{3,2,1,0:T(8,128)}, u32[]{:S(2)}) copy-start(f32[3,2,16,16]{3,2,1,0:T(8,128)} %rows.5) | copy-start | bytes 18436
  2.4 0.8 %copy-start.11 = (f32[3,2,16,16]{3,2,1,0:T(8,128)S(1)}, f32[3,2,16,16]{3,2,1,0:T(8,128)}, u32[]{:S(2)}) copy-start(f32[3,2,16,16]{3,2,1,0:T(8,128)} %cols.5) | copy-start | bytes 18436
  3.2 0.7 %copy-start.14 = (f32[3,2,2,1,256]{4,3,2,1,0:T(1,128)S(1)}, f32[3,2,2,1,256]{4,3,2,1,0:T(1,128)}, u32[]{:S(2)}) copy-start(f32[3,2,2,1,256]{4,3,2,1,0:T(1,128)} %sources.5) | copy-start | bytes 36868
  8.5 16.7 %all-to-all-start = ((f32[4,64,256]{2,1,0:T(8,128)}), f32[4,64,256]{2,1,0:T(8,128)S(1)}, u32[]{:S(2)}, u32[]{:S(2)}) async-start(f32[4,64,256]{2,1,0:T(8,128)} %first.1), calls=%async_computation | async-start | bytes 524288 | tf_op jit(solution)/shard_map/all_to_all | solution.py:169
  17.8 0.8 %copy-start.6 = (f32[3,2,2,2,2,1,256]{6,5,4,3,2,1,0:T(1,128)S(1)}, f32[3,2,2,2,2,1,256]{6,5,4,3,2,1,0:T(1,128)}, u32[]{:S(2)}) copy-start(f32[3,2,2,2,2,1,256]{6,5,4,3,2,1,0:T(1,128)} %targets.5) | copy-start | bytes 147460
  18.6 0.8 %copy-start.9 = (f32[3,2,16,16]{3,2,1,0:T(8,128)S(1)}, f32[3,2,16,16]{3,2,1,0:T(8,128)}, u32[]{:S(2)}) copy-start(f32[3,2,16,16]{3,2,1,0:T(8,128)} %rows.5) | copy-start | bytes 18436
  19.4 0.8 %copy-start.12 = (f32[3,2,16,16]{3,2,1,0:T(8,128)S(1)}, f32[3,2,16,16]{3,2,1,0:T(8,128)}, u32[]{:S(2)}) copy-start(f32[3,2,16,16]{3,2,1,0:T(8,128)} %cols.5) | copy-start | bytes 18436
  20.2 0.7 %copy-start.15 = (f32[3,2,2,1,256]{4,3,2,1,0:T(1,128)S(1)}, f32[3,2,2,1,256]{4,3,2,1,0:T(1,128)}, u32[]{:S(2)}) copy-start(f32[3,2,2,1,256]{4,3,2,1,0:T(1,128)} %sources.5) | copy-start | bytes 36868
  23.9 1.3 %copy-start = (bf16[8,512,256]{2,1,0:T(8,128)(2,1)}, bf16[8,512,256]{2,1,0:T(8,128)(2,1)S(1)}, u32[]{:S(2)}) copy-start(bf16[8,512,256]{2,1,0:T(8,128)(2,1)S(1)} %get-tuple-element.10.low) | copy-start | bytes 6291460
  25.3 1.6 %copy-start.1 = (bf16[8,512,256]{2,1,0:T(8,128)(2,1)S(1)}, bf16[8,512,256]{2,1,0:T(8,128)(2,1)}, u32[]{:S(2)}) copy-start(bf16[8,512,256]{2,1,0:T(8,128)(2,1)} %copy-done) | copy-start | bytes 6291460
  26.9 5.0 %copy-start.7 = (f32[3,2,2,2,2,1,256]{6,5,4,3,2,1,0:T(1,128)S(1)}, f32[3,2,2,2,2,1,256]{6,5,4,3,2,1,0:T(1,128)}, u32[]{:S(2)}) copy-start(f32[3,2,2,2,2,1,256]{6,5,4,3,2,1,0:T(1,128)} %targets.5) | copy-start | bytes 147460
  26.9 5.0 %copy-start.10 = (f32[3,2,16,16]{3,2,1,0:T(8,128)S(1)}, f32[3,2,16,16]{3,2,1,0:T(8,128)}, u32[]{:S(2)}) copy-start(f32[3,2,16,16]{3,2,1,0:T(8,128)} %rows.5) | copy-start | bytes 18436
  26.9 5.0 %copy-start.13 = (f32[3,2,16,16]{3,2,1,0:T(8,128)S(1)}, f32[3,2,16,16]{3,2,1,0:T(8,128)}, u32[]{:S(2)}) copy-start(f32[3,2,16,16]{3,2,1,0:T(8,128)} %cols.5) | copy-start | bytes 18436
  26.9 5.0 %copy-start.16 = (f32[3,2,2,1,256]{4,3,2,1,0:T(1,128)S(1)}, f32[3,2,2,1,256]{4,3,2,1,0:T(1,128)}, u32[]{:S(2)}) copy-start(f32[3,2,2,1,256]{4,3,2,1,0:T(1,128)} %sources.5) | copy-start | bytes 36868
  28.4 9.3 %all-to-all-start.1 = ((f32[4,64,256]{2,1,0:T(8,128)}), f32[4,64,256]{2,1,0:T(8,128)S(1)}, u32[]{:S(2)}, u32[]{:S(2)}) async-start(f32[4,64,256]{2,1,0:T(8,128)} %later_1.1), calls=%async_computation.1 | async-start | bytes 524288 | tf_op jit(solution)/shard_map/all_to_all | solution.py:169
  35.0 1.3 %copy-start.2 = (bf16[8,512,256]{2,1,0:T(8,128)(2,1)}, bf16[8,512,256]{2,1,0:T(8,128)(2,1)S(1)}, u32[]{:S(2)}) copy-start(bf16[8,512,256]{2,1,0:T(8,128)(2,1)S(1)} %get-tuple-element.12.low) | copy-start | bytes 6291460
  37.7 1.6 %copy-start.3 = (bf16[8,512,256]{2,1,0:T(8,128)(2,1)S(1)}, bf16[8,512,256]{2,1,0:T(8,128)(2,1)}, u32[]{:S(2)}) copy-start(bf16[8,512,256]{2,1,0:T(8,128)(2,1)} %copy-done.2) | copy-start | bytes 6291460
